TPU v7x, 32 devices: a whole 2x2x4 slice. The times are simulated.
32 devices in a mesh: dp: 8 (over z, y), tensor: 4 (over x, core).
Axes of the slice: x: 2, y: 2, z: 4, core: 2. Of those that a mesh axis runs over, the one named last changes fastest.
Arguments:
- attn_out: bfloat16 [2048, 4096], P('dp', 'tensor'), may hold values from -6 to 6
- w_blocks: bfloat16 [4096, 8192], P('tensor', 'dp'), may hold values from -0.09375 to 0.09375
- w_scales: float32 [32, 8192], P('tensor', 'dp'), may hold values from 0.5 to 2
- residual: bfloat16 [2048, 8192], P('dp')
- gain: float32 [8192], P('tensor'), may hold values from 0.5 to 1.5
Outputs:
- hidden: bfloat16 [2048, 8192], P('dp', 'tensor')
- normed: bfloat16 [2048, 8192], P('dp', 'tensor')
All inputs are finite; a program needn't handle non-finite values.
Results may differ from a plain program's by a relative error of at most 0.014.
Values may be sent and summed in bfloat16 or wider, within the bound.
A program may use at most 128 MiB of HBM per device.

v0:
```python
import functools

import jax
import jax.numpy as jnp
from jax import lax
from jax.experimental import pallas as pl
from jax.experimental.pallas import tpu as pltpu
from jax.sharding import PartitionSpec as P

MESH = pl.DeviceIdType.MESH
WIDTH = 256
LANES = 128


def plan(dp, groups, cols):
    inner = dp // groups
    width = min(WIDTH, cols)
    own = cols // width
    peers = (inner - 1) * own
    wave_of_seg = [0] * own + [1 + p * groups // peers for p in range(peers)]
    waves = [[] for _ in range(groups + 1)]
    for j in range(groups):
        for s, at in enumerate(wave_of_seg):
            waves[max(j, at)].append((j, s))
    return inner, width, own, wave_of_seg, waves


def kernel(
    dp, groups,
    a_ref, w_ref, sc_ref, res_hbm,
    hidden_ref, scl,
    a_buf, w_buf, sc_buf, wd, res, part,
    snd1, rcv1, keep2, snd2, rcv2, snd3, zin, hs, acc, scl_snd,
    res_sem, a_send, a_recv, w_send, w_recv, sc_send, sc_recv,
    s1, r1, s2, r2, s3, r3, s4, r4, s5, r5,
):
    rows, depth = a_ref.shape
    cols = w_ref.shape[1]
    my_cols = hidden_ref.shape[1]
    blocks = sc_ref.shape[0]
    per_block = depth // blocks
    half, quarter = rows // 2, rows // 4
    inner, width, own, wave_of_seg, waves = plan(dp, groups, cols)
    segs = len(wave_of_seg)

    d = lax.axis_index("dp")
    t = lax.axis_index("tensor")
    z, i = d // inner, d % inner
    core, x = t % 2, t // 2
    core_peer = t + 1 - 2 * core
    x_peer = (t + 2) % 4

    def line(o):
        return {"dp": o * inner + i, "tensor": t}

    def row(other):
        return {"dp": d, "tensor": other}

    def pair(other):
        return {"dp": z * inner + other, "tensor": t}

    def step_block(j):
        if j == 0:
            return z
        if j == 1:
            return z + 1 - 2 * (z % 2)
        if j == 2:
            return z + 2 - 4 * (z // 2)
        return 3 - z

    def row_offset(who):
        return pl.multiple_of((who % 2) * half + (who // 2) * quarter, quarter)

    def seg_col(s):
        return pl.multiple_of(((i + s // own) % inner) * cols + (s % own) * width, width)

    def remote(src, dst, send, recv, to):
        return pltpu.make_async_remote_copy(
            src_ref=src, dst_ref=dst, send_sem=send, recv_sem=recv,
            device_id=to, device_id_type=MESH,
        )

    mine = row_offset(t)
    res_copy = pltpu.make_async_copy(res_hbm.at[pl.ds(mine, quarter), :], res, res_sem)
    res_copy.start()

    barrier = pltpu.get_barrier_semaphore()
    for r in range(1, inner):
        pl.semaphore_signal(barrier, inc=1, device_id=pair((i + r) % inner), device_id_type=MESH)
    for r in range(1, groups):
        pl.semaphore_signal(barrier, inc=1, device_id=line((z + r) % groups), device_id_type=MESH)
    for r in range(1, 4):
        pl.semaphore_signal(barrier, inc=1, device_id=row((t + r) % 4), device_id_type=MESH)
    pl.semaphore_wait(barrier, inner - 1 + groups - 1 + 3)

    def a_copy(src, block, send, to):
        return remote(src, a_buf.at[block], a_send.at[send], a_recv.at[block], line(to))

    @pl.when(z < groups - 1)
    def _():
        a_copy(a_ref, z, z, z + 1).start()

    @pl.when(z > 0)
    def _():
        a_copy(a_ref, z, groups, z - 1).start()

    def sc_copy(r):
        return remote(sc_ref, sc_buf.at[r - 1], sc_send.at[r - 1], sc_recv.at[r - 1], pair((i + inner - r) % inner))

    def w_copy(r, c):
        k = (r - 1) * own + c
        return remote(
            w_ref.at[:, pl.ds(c * width, width)], w_buf.at[k], w_send.at[k], w_recv.at[k],
            pair((i + inner - r) % inner),
        )

    for r in range(1, inner):
        sc_copy(r).start()
    for r in range(1, inner):
        for c in range(own):
            w_copy(r, c).start()

    def dequantize(s):
        c = s % own
        for b in range(blocks):
            lines = pl.ds(b * per_block, per_block)
            if s < own:
                raw = w_ref[lines, pl.ds(c * width, width)]
                scale = sc_ref[pl.ds(b, 1), pl.ds(c * width, width)]
            else:
                raw = w_buf[s - own, lines, :]
                scale = sc_buf[s // own - 1, pl.ds(b, 1), pl.ds(c * width, width)]
            wd[s, lines, :] = (raw.astype(jnp.float32) * scale).astype(jnp.bfloat16)

    def forward(k):
        @pl.when(z >= k)
        def _():
            b = z - k
            a_copy(a_ref, b, b, z).wait_recv()

            @pl.when(z < groups - 1)
            def _():
                a_copy(a_buf.at[b], b, b, z + 1).start()

        @pl.when(z + k <= groups - 1)
        def _():
            b = z + k
            a_copy(a_ref, b, b, z).wait_recv()

            @pl.when(z > 0)
            def _():
                a_copy(a_buf.at[b], b, b, z - 1).start()

    def copy1(u):
        return remote(snd1.at[u], rcv1.at[u], s1.at[u], r1.at[u], row(core_peer))

    def copy2(u):
        return remote(snd2.at[u], rcv2.at[u], s2.at[u], r2.at[u], row(x_peer))

    def copy3(u, j):
        return remote(snd3.at[u], zin.at[u], s3.at[u], r3.at[u], line(step_block(j)))

    def copy4(u, j, s):
        return remote(
            hs.at[u], hidden_ref.at[pl.ds(mine, quarter), pl.ds(seg_col(s), width)],
            s4.at[u], r4.at[t * segs + s], row(step_block(j)),
        )

    keep_rows = pl.multiple_of(core * half, half)
    send_rows = pl.multiple_of((1 - core) * half, half)

    def stage1(u, j, s):
        a = a_ref[...] if j == 0 else a_buf[step_block(j)]
        part[u % 2] = jnp.dot(a, wd[s], preferred_element_type=jnp.float32)
        snd1[u] = part[u % 2, pl.ds(send_rows, half), :].astype(jnp.bfloat16)
        copy1(u).start()

    def stage2(u):
        copy1(u).wait_recv()
        near = pl.multiple_of(x * quarter, quarter)
        far = pl.multiple_of((1 - x) * quarter, quarter)
        snd2[u] = (
            part[u % 2, pl.ds(pl.multiple_of(keep_rows + far, quarter), quarter), :]
            + rcv1[u, pl.ds(far, quarter), :].astype(jnp.float32)
        ).astype(jnp.bfloat16)
        copy2(u).start()
        keep2[u] = (
            part[u % 2, pl.ds(pl.multiple_of(keep_rows + near, quarter), quarter), :]
            + rcv1[u, pl.ds(near, quarter), :].astype(jnp.float32)
        )

    def stage3(u, j):
        copy2(u).wait_recv()
        total = (keep2[u] + rcv2[u].astype(jnp.float32)).astype(jnp.bfloat16)
        if j == 0:
            zin[u] = total
        else:
            snd3[u] = total
            copy3(u, j).start()

    def stage4(u, j, s):
        if j > 0:
            copy3(u, j).wait_recv()
        source = step_block(j)
        at = pl.multiple_of(source * my_cols + seg_col(s), width)
        h = (zin[u].astype(jnp.float32) + res[:, pl.ds(at, width)].astype(jnp.float32)).astype(jnp.bfloat16)
        hs[u] = h

        @pl.when(source != t)
        def _():
            copy4(u, j, s).start()

        @pl.when(source == t)
        def _():
            hidden_ref[pl.ds(mine, quarter), pl.ds(seg_col(s), width)] = hs[u]

        wide = h.astype(jnp.float32)
        square = wide * wide
        total = acc[...]
        for k in range(width // LANES):
            total = total + square[:, k * LANES:(k + 1) * LANES]
        acc[...] = total

    acc[...] = jnp.zeros_like(acc)
    number = 0
    late = []
    units = []
    for w, wave in enumerate(waves):
        if 1 <= w < groups:
            forward(w)
        for s in range(segs):
            if wave_of_seg[s] == w:
                if s >= own:
                    r, c = s // own, s % own
                    if c == 0:
                        sc_copy(r).wait_recv()
                    w_copy(r, c).wait_recv()
                dequantize(s)
        now = [(number + k, j, s) for k, (j, s) in enumerate(wave)]
        number += len(wave)
        for k, (u, j, s) in enumerate(now):
            stage1(u, j, s)
            if k > 0:
                stage2(now[k - 1][0])
        if now:
            stage2(now[-1][0])
        if w == 1:
            res_copy.wait()
        for u, j, s in late:
            stage4(u, j, s)
        for u, j, s in now:
            stage3(u, j)
        late = now
        units += now
    for u, j, s in late:
        stage4(u, j, s)

    mean_square = jnp.sum(acc[...], axis=1, keepdims=True) / (my_cols * groups)
    scl_snd[...] = jnp.broadcast_to(lax.rsqrt(mean_square + 1e-05), scl_snd.shape)
    scl[pl.ds(mine, quarter), :] = scl_snd[...]

    def copy5(r):
        return remote(
            scl_snd, scl.at[pl.ds(mine, quarter), :], s5.at[r - 1], r5.at[t], row((t + r) % 4)
        )

    for r in range(1, 4):
        copy5(r).start()

    for r in range(1, 4):
        who = (t + r) % 4
        at = pl.ds(row_offset(who), quarter)
        for s in range(segs):
            piece = hidden_ref.at[at, pl.ds(seg_col(s), width)]
            remote(hs.at[0], piece, s4.at[0], r4.at[who * segs + s], row(who)).wait_recv()
        remote(scl_snd, scl.at[at, :], s5.at[0], r5.at[who], row(who)).wait_recv()

    @pl.when(z < groups - 1)
    def _():
        a_copy(a_ref, z, z, z + 1).wait_send()

    @pl.when(z > 0)
    def _():
        a_copy(a_ref, z, groups, z - 1).wait_send()

    for k in range(1, groups):
        @pl.when((z >= k) & (z < groups - 1))
        def _():
            a_copy(a_ref, z - k, z - k, z + 1).wait_send()

        @pl.when((z + k <= groups - 1) & (z > 0))
        def _():
            a_copy(a_ref, z + k, z + k, z - 1).wait_send()

    for r in range(1, inner):
        sc_copy(r).wait_send()
        for c in range(own):
            w_copy(r, c).wait_send()
    for u, j, s in units:
        copy1(u).wait_send()
        copy2(u).wait_send()
        if j > 0:
            copy3(u, j).wait_send()

        @pl.when(step_block(j) != t)
        def _():
            copy4(u, j, s).wait_send()
    for r in range(1, 4):
        copy5(r).wait_send()


def solution(mesh):
    dp, groups = mesh.shape["dp"], mesh.shape["tensor"]

    def on_device(attn_out, w_blocks, w_scales, residual, gain):
        rows, depth = attn_out.shape
        cols = w_blocks.shape[1]
        my_cols = gain.shape[0]
        inner, width, own, wave_of_seg, waves = plan(dp, groups, cols)
        segs = len(wave_of_seg)
        n = segs * groups
        peers = segs - own
        half, quarter = rows // 2, rows // 4
        bf16, f32 = jnp.bfloat16, jnp.float32
        vmem = pl.BlockSpec(memory_space=pltpu.VMEM)
        dma = pltpu.SemaphoreType.DMA
        out = jax.ShapeDtypeStruct((rows, my_cols), bf16)
        hidden, scale = pl.pallas_call(
            functools.partial(kernel, dp, groups),
            out_shape=(out, jax.ShapeDtypeStruct((rows, LANES), f32)),
            in_specs=[vmem, vmem, vmem, pl.BlockSpec(memory_space=pl.ANY)],
            out_specs=(vmem, vmem),
            scratch_shapes=[
                pltpu.VMEM((groups, rows, depth), bf16),
                pltpu.VMEM((peers, depth, width), bf16),
                pltpu.VMEM((inner - 1,) + w_scales.shape, f32),
                pltpu.VMEM((segs, depth, width), bf16),
                pltpu.VMEM((quarter, residual.shape[1]), bf16),
                pltpu.VMEM((2, rows, width), f32),
                pltpu.VMEM((n, half, width), bf16),
                pltpu.VMEM((n, half, width), bf16),
                pltpu.VMEM((n, quarter, width), f32),
                pltpu.VMEM((n, quarter, width), bf16),
                pltpu.VMEM((n, quarter, width), bf16),
                pltpu.VMEM((n, quarter, width), bf16),
                pltpu.VMEM((n, quarter, width), bf16),
                pltpu.VMEM((n, quarter, width), bf16),
                pltpu.VMEM((quarter, LANES), f32),
                pltpu.VMEM((quarter, LANES), f32),
                dma, dma((groups + 1,)), dma((groups,)), dma((peers,)), dma((peers,)),
                dma((inner - 1,)), dma((inner - 1,)),
                dma((n,)), dma((n,)), dma((n,)), dma((n,)), dma((n,)), dma((n,)),
                dma((n,)), dma((groups * segs,)), dma((3,)), dma((groups,)),
            ],
            compiler_params=pltpu.CompilerParams(
                collective_id=0, has_side_effects=True, vmem_limit_bytes=60 * 1024 * 1024,
            ),
        )(attn_out, w_blocks, w_scales, residual)
        normed = (hidden.astype(f32) * gain[None, :] * scale[:, :1]).astype(bf16)
        return hidden, normed

    return jax.shard_map(
        on_device,
        mesh=mesh,
        in_specs=(
            P("dp", "tensor"),
            P("tensor", "dp"),
            P("tensor", "dp"),
            P("dp", None),
            P("tensor"),
        ),
        out_specs=(P("dp", "tensor"), P("dp", "tensor")),
        check_vma=False,
    )
```

profile of v0, /device:TPU:0, one launch (start us, length us, event | category | flops | bytes accessed | tf_op | source)
XLA Modules:
  0.0 85.6 jit_solution(17127581259740803568)
XLA Ops:
  0.6 0.0 copy-start.1
  0.6 80.4 %shard_map.68 = (bf16[256,2048]{1,0:T(8,128)(2,1)}, f32[256,128]{1,0:T(8,128)}) custom-call(bf16[256,1024]{1,0:T(8,128)(2,1)} %a_ref.1, bf16[1024,1024]{1,0:T(8,128)(2,1)} %w_ref.1, f32[8,1024]{1,0:T(8,128)} %sc_ref.1, bf16[256,8192]{1,0:T(8,128)(2,1)} %res_hbm.1), custom_call_target="tpu_custom_call" | custom-call | tf_op jit(solution)/shard_map/pallas_call | solution.py:328
  81.0 0.0 copy-start
  81.0 1.1 %slice_reduce_fusion = f32[256]{0:T(256)S(1)} fusion(f32[256,128]{1,0:T(8,128)} %get-tuple-element.5), kind=kLoop, calls=%fused_computation.1 | loop fusion | bytes 2048 | tf_op jit(solution)/shard_map/slice | solution.py:359
  82.1 0.0 copy-done.1
  82.1 2.5 %multiply_convert_fusion = bf16[256,2048]{1,0:T(8,128)(2,1)} fusion(bf16[256,2048]{1,0:T(8,128)(2,1)} %get-tuple-element.8, f32[256]{0:T(256)S(1)} %slice_reduce_fusion, f32[2048]{0:T(1024)S(1)} %copy-done.1), kind=kLoop, calls=%fused_computation | loop fusion | flops 2097152 | bytes 2106368 | tf_op jit(solution)/shard_map/convert_element_type | solution.py:359
  84.6 0.0 copy-done
  84.6 1.0 %copy.8 = bf16[256,2048]{1,0:T(8,128)(2,1)} copy(bf16[256,2048]{1,0:T(8,128)(2,1)S(1)} %copy-done) | data formatting | bytes 2097152
Async XLA Ops:
  0.6 81.5 %copy-start.1 = (f32[2048]{0:T(1024)S(1)}, f32[2048]{0:T(1024)}, u32[]{:S(2)}) copy-start(f32[2048]{0:T(1024)} %param.9) | copy-start | bytes 24580
  81.0 3.6 %copy-start = (bf16[256,2048]{1,0:T(8,128)(2,1)S(1)}, bf16[256,2048]{1,0:T(8,128)(2,1)}, u32[]{:S(2)}) copy-start(bf16[256,2048]{1,0:T(8,128)(2,1)} %get-tuple-element.8) | copy-start | bytes 3145732
where the time goes:
time: 85.8 us; the launch traced here: 85.6 us
  Pallas kernels  80.4 us (94%)
  other arithmetic  2.46 us (3%)
  local copies, waits for them, and re-layouts  2.07 us (2%)
    pallas_call x1, Pallas kernels, on_device(): pl.pallas_call(functools.partial(kernel, dp, groups), out_shape=(out, jax...  80.4 us
    convert_element_type x1, other arithmetic, on_device(): normed = (hidden.astype(f32) * gain[None, :] * scale[:, :1]).astype(bf16)  2.46 us

commit v1 on v0

v1 whole, which is shorter than its diff:
```python
import functools

import jax
import jax.numpy as jnp
from jax import lax
from jax.experimental import pallas as pl
from jax.experimental.pallas import tpu as pltpu
from jax.sharding import PartitionSpec as P

MESH = pl.DeviceIdType.MESH
WIDTH = 256
LANES = 128
PARTS = 2


def plan(dp, groups, cols):
    inner = dp // groups
    width = min(WIDTH, cols)
    pieces = [(0, c, width) for c in range(0, cols, width)]
    own = len(pieces)
    for r in range(1, inner):
        for c in range(0, cols, width):
            if r == inner - 1 and c == cols - width and width > LANES:
                pieces += [(r, k, LANES) for k in range(c, cols, LANES)]
            else:
                pieces.append((r, c, width))
    total = (inner - 1) * cols
    level, done = [0] * own, 0
    for _, _, w in pieces[own:]:
        done += w
        level.append(1 + (done * groups - 1) // total)
    last = [s for s, at in enumerate(level) if at >= groups]
    for k, s in enumerate(last):
        level[s] = groups + (2 * k) // len(last)
    waves = [[] for _ in range(groups + 2)]
    for j in range(groups):
        for s, at in enumerate(level):
            waves[max(j, at)].append((j, s))
    return inner, width, pieces, own, level, waves


def kernel(
    dp, groups,
    a_hbm, w_hbm, sc_hbm, res_hbm,
    hidden, scl,
    a_buf, w_buf, sc_buf, wd, res,
    keep1, snd1, rcv1, snd2, keep2, rcv2, snd3, zin, hs, acc, scl_snd,
    a_load, w_load, sc_load, res_load,
    a_send, a_recv, w_send, w_recv, sc_send, sc_recv,
    s1, r1, s2, r2, s3, r3, s4, r4, s5, r5,
):
    rows, depth = a_hbm.shape
    cols = w_hbm.shape[1]
    my_cols = hidden.shape[1]
    blocks = sc_hbm.shape[0]
    per_block = depth // blocks
    half, quarter = rows // 2, rows // 4
    inner, width, pieces, own, level, waves = plan(dp, groups, cols)
    segs = len(pieces)

    d = lax.axis_index("dp")
    t = lax.axis_index("tensor")
    z, i = d // inner, d % inner
    core, x = t % 2, t // 2
    core_peer = t + 1 - 2 * core
    x_peer = (t + 2) % 4

    def line(o):
        return {"dp": o * inner + i, "tensor": t}

    def row(other):
        return {"dp": d, "tensor": other}

    def pair(other):
        return {"dp": z * inner + other, "tensor": t}

    def step_block(j):
        if j == 0:
            return z
        if j == 1:
            return z + 1 - 2 * (z % 2)
        if j == 2:
            return z + 2 - 4 * (z // 2)
        return 3 - z

    def row_offset(who):
        return pl.multiple_of((who % 2) * half + (who // 2) * quarter, quarter)

    def seg_col(s):
        r, c, w = pieces[s]
        return pl.multiple_of(((i + r) % inner) * cols + c, w)

    def remote(src, dst, send, recv, to):
        return pltpu.make_async_remote_copy(
            src_ref=src, dst_ref=dst, send_sem=send, recv_sem=recv,
            device_id=to, device_id_type=MESH,
        )

    mine = row_offset(t)
    order = [t, x_peer, core_peer, (core_peer + 2) % 4]

    def load_a(q):
        return pltpu.make_async_copy(
            a_hbm.at[pl.ds(row_offset(order[q]), quarter), :],
            a_buf.at[z, pl.ds(q * quarter, quarter), :], a_load.at[q],
        )

    def load_w(s):
        _, c, w = pieces[s]
        return pltpu.make_async_copy(w_hbm.at[:, pl.ds(c, w)], w_buf.at[s, :, pl.ds(0, w)], w_load.at[s])

    sc_copy_in = pltpu.make_async_copy(sc_hbm, sc_buf.at[0], sc_load)
    res_copy = pltpu.make_async_copy(res_hbm.at[pl.ds(mine, quarter), :], res, res_load)
    for q in range(4):
        load_a(q).start()
    sc_copy_in.start()
    for s in range(own):
        load_w(s).start()
    res_copy.start()

    barrier = pltpu.get_barrier_semaphore()
    for r in range(1, inner):
        pl.semaphore_signal(barrier, inc=1, device_id=pair((i + r) % inner), device_id_type=MESH)
    for r in range(1, groups):
        pl.semaphore_signal(barrier, inc=1, device_id=line((z + r) % groups), device_id_type=MESH)
    for r in range(1, 4):
        pl.semaphore_signal(barrier, inc=1, device_id=row((t + r) % 4), device_id_type=MESH)
    pl.semaphore_wait(barrier, inner - 1 + groups - 1 + 3)

    size = rows // PARTS

    def a_copy(block, h, send, to):
        part = a_buf.at[block, pl.ds(h * size, size), :]
        return remote(part, part, a_send.at[send, h], a_recv.at[block, h], line(to))

    def sc_copy(r):
        return remote(sc_buf.at[0], sc_buf.at[r], sc_send.at[r - 1], sc_recv.at[r - 1], pair((i + inner - r) % inner))

    def w_copy(s):
        r, c, w = pieces[s]
        k, at = c // width, c % width
        return remote(
            w_buf.at[k, :, pl.ds(at, w)], w_buf.at[s, :, pl.ds(0, w)], w_send.at[s - own], w_recv.at[s - own],
            pair((i + inner - r) % inner),
        )

    for q in range(4):
        load_a(q).wait()
    for h in range(PARTS):
        @pl.when(z < groups - 1)
        def _():
            a_copy(z, h, z, z + 1).start()

        @pl.when(z > 0)
        def _():
            a_copy(z, h, groups, z - 1).start()

    sc_copy_in.wait()
    for r in range(1, inner):
        sc_copy(r).start()
    for s in range(own):
        load_w(s).wait()
    for s in range(own, segs):
        w_copy(s).start()

    def dequantize(s):
        r, c, w = pieces[s]
        for b in range(blocks):
            lines = pl.ds(b * per_block, per_block)
            raw = w_buf[s, lines, pl.ds(0, w)]
            scale = sc_buf[r, pl.ds(b, 1), pl.ds(c, w)]
            wd[s, lines, pl.ds(0, w)] = (raw.astype(jnp.float32) * scale).astype(jnp.bfloat16)

    def forward(k, h):
        @pl.when(z >= k)
        def _():
            b = z - k
            a_copy(b, h, b, z).wait_recv()

            @pl.when(z < groups - 1)
            def _():
                a_copy(b, h, b, z + 1).start()

        @pl.when(z + k <= groups - 1)
        def _():
            b = z + k
            a_copy(b, h, b, z).wait_recv()

            @pl.when(z > 0)
            def _():
                a_copy(b, h, b, z - 1).start()

    units = [unit for wave in waves for unit in wave]

    def piece(ref, u):
        return ref.at[u, :, pl.ds(0, pieces[units[u][1]][2])]

    def copy1(u):
        return remote(piece(snd1, u), piece(rcv1, u), s1.at[u], r1.at[u], row(core_peer))

    def copy2(u):
        return remote(piece(snd2, u), piece(rcv2, u), s2.at[u], r2.at[u], row(x_peer))

    def copy3(u):
        return remote(piece(snd3, u), piece(zin, u), s3.at[u], r3.at[u], line(step_block(units[u][0])))

    def place(who, s):
        return hidden.at[pl.ds(row_offset(who), quarter), pl.ds(seg_col(s), pieces[s][2])]

    def copy4(u):
        j, s = units[u]
        return remote(piece(hs, u), place(t, s), s4.at[u], r4.at[t * segs + s], row(step_block(j)))

    def keep4(u):
        return pltpu.make_async_copy(piece(hs, u), place(t, units[u][1]), s4.at[u])

    def stage1(u):
        j, s = units[u]
        w = pieces[s][2]
        part = jnp.dot(a_buf[step_block(j)], wd[s, :, pl.ds(0, w)], preferred_element_type=jnp.float32)
        snd1[u, :, pl.ds(0, w)] = part[half:].astype(jnp.bfloat16)
        copy1(u).start()
        keep1[u, :, pl.ds(0, w)] = part[:half]

    def stage2(u):
        w = pieces[units[u][1]][2]
        copy1(u).wait_recv()
        total = keep1[u, :, pl.ds(0, w)] + rcv1[u, :, pl.ds(0, w)].astype(jnp.float32)
        snd2[u, :, pl.ds(0, w)] = total[quarter:].astype(jnp.bfloat16)
        copy2(u).start()
        keep2[u, :, pl.ds(0, w)] = total[:quarter]

    def stage3(u):
        j, s = units[u]
        w = pieces[s][2]
        copy2(u).wait_recv()
        total = (keep2[u, :, pl.ds(0, w)] + rcv2[u, :, pl.ds(0, w)].astype(jnp.float32)).astype(jnp.bfloat16)
        if j == 0:
            zin[u, :, pl.ds(0, w)] = total
        else:
            snd3[u, :, pl.ds(0, w)] = total
            copy3(u).start()

    def stage4(u):
        j, s = units[u]
        w = pieces[s][2]
        if j > 0:
            copy3(u).wait_recv()
        source = step_block(j)
        at = pl.multiple_of(source * my_cols + seg_col(s), w)
        h = (zin[u, :, pl.ds(0, w)].astype(jnp.float32) + res[:, pl.ds(at, w)].astype(jnp.float32)).astype(jnp.bfloat16)
        hs[u, :, pl.ds(0, w)] = h

        @pl.when(source != t)
        def _():
            copy4(u).start()

        @pl.when(source == t)
        def _():
            keep4(u).start()

        wide = h.astype(jnp.float32)
        square = wide * wide
        total = acc[...]
        for k in range(w // LANES):
            total = total + square[:, k * LANES:(k + 1) * LANES]
        acc[...] = total

    acc[...] = jnp.zeros_like(acc)
    number = 0
    late = []

    def weights(at):
        for s in range(segs):
            if level[s] == at:
                r = pieces[s][0]
                if r > 0:
                    if pieces[s - 1][0] != r:
                        sc_copy(r).wait_recv()
                    w_copy(s).wait_recv()
                dequantize(s)

    for n, wave in enumerate(waves):
        now = list(range(number, number + len(wave)))
        number += len(wave)
        if 1 <= n < groups:
            forward(n, PARTS - 1)
        weights(n)
        for u in now:
            stage1(u)
        for u in now:
            stage2(u)
        if n == 0:
            res_copy.wait()
        if n + 1 < groups:
            for h in range(PARTS - 1):
                forward(n + 1, h)
        for u in now:
            stage3(u)
        for u in late:
            stage4(u)
        late = now
    for u in late:
        stage4(u)

    mean_square = jnp.sum(acc[...], axis=1, keepdims=True) / (my_cols * groups)
    scl_snd[...] = jnp.broadcast_to(lax.rsqrt(mean_square + 1e-05), scl_snd.shape)
    keep5 = pltpu.make_async_copy(scl_snd, scl.at[pl.ds(mine, quarter), :], s5.at[3])

    def copy5(r):
        return remote(
            scl_snd, scl.at[pl.ds(mine, quarter), :], s5.at[r - 1], r5.at[t], row((t + r) % 4)
        )

    for r in range(1, 4):
        copy5(r).start()
    keep5.start()

    @pl.when(z < groups - 1)
    def _():
        for h in range(PARTS):
            a_copy(z, h, z, z + 1).wait_send()

    @pl.when(z > 0)
    def _():
        for h in range(PARTS):
            a_copy(z, h, groups, z - 1).wait_send()

    for k in range(1, groups):
        @pl.when((z >= k) & (z < groups - 1))
        def _():
            for h in range(PARTS):
                a_copy(z - k, h, z - k, z + 1).wait_send()

        @pl.when((z + k <= groups - 1) & (z > 0))
        def _():
            for h in range(PARTS):
                a_copy(z + k, h, z + k, z - 1).wait_send()

    for r in range(1, inner):
        sc_copy(r).wait_send()
    for s in range(own, segs):
        w_copy(s).wait_send()
    for u, (j, s) in enumerate(units):
        copy1(u).wait_send()
        copy2(u).wait_send()
        if j > 0:
            copy3(u).wait_send()

    for r in range(1, 4):
        who = (t + r) % 4
        for s in range(segs):
            w = pieces[s][2]
            remote(hs.at[0, :, pl.ds(0, w)], place(who, s), s4.at[0], r4.at[who * segs + s], row(who)).wait_recv()
    for u, (j, s) in enumerate(units):
        @pl.when(step_block(j) != t)
        def _():
            copy4(u).wait_send()

        @pl.when(step_block(j) == t)
        def _():
            keep4(u).wait()
    for r in range(1, 4):
        who = (t + r) % 4
        remote(scl_snd, scl.at[pl.ds(row_offset(who), quarter), :], s5.at[0], r5.at[who], row(who)).wait_recv()
    for r in range(1, 4):
        copy5(r).wait_send()
    keep5.wait()


def finish(h_ref, scale_ref, gain_ref, hidden_ref, normed_ref):
    h = h_ref[...]
    hidden_ref[...] = h
    normed_ref[...] = (h.astype(jnp.float32) * gain_ref[...] * scale_ref[:, :1]).astype(jnp.bfloat16)


def solution(mesh):
    dp, groups = mesh.shape["dp"], mesh.shape["tensor"]

    def on_device(attn_out, w_blocks, w_scales, residual, gain):
        rows, depth = attn_out.shape
        cols = w_blocks.shape[1]
        my_cols = gain.shape[0]
        inner, width, pieces, own, level, waves = plan(dp, groups, cols)
        segs = len(pieces)
        n = segs * groups
        peers = segs - own
        half, quarter = rows // 2, rows // 4
        bf16, f32 = jnp.bfloat16, jnp.float32
        hbm = pl.BlockSpec(memory_space=pl.ANY)
        dma = pltpu.SemaphoreType.DMA
        out = jax.ShapeDtypeStruct((rows, my_cols), bf16)
        hidden, scale = pl.pallas_call(
            functools.partial(kernel, dp, groups),
            out_shape=(out, jax.ShapeDtypeStruct((rows, LANES), f32)),
            in_specs=[hbm] * 4,
            out_specs=(hbm, hbm),
            scratch_shapes=[
                pltpu.VMEM((groups, rows, depth), bf16),
                pltpu.VMEM((segs, depth, width), bf16),
                pltpu.VMEM((inner,) + w_scales.shape, f32),
                pltpu.VMEM((segs, depth, width), bf16),
                pltpu.VMEM((quarter, residual.shape[1]), bf16),
                pltpu.VMEM((n, half, width), f32),
                pltpu.VMEM((n, half, width), bf16),
                pltpu.VMEM((n, half, width), bf16),
                pltpu.VMEM((n, quarter, width), bf16),
                pltpu.VMEM((n, quarter, width), f32),
                pltpu.VMEM((n, quarter, width), bf16),
                pltpu.VMEM((n, quarter, width), bf16),
                pltpu.VMEM((n, quarter, width), bf16),
                pltpu.VMEM((n, quarter, width), bf16),
                pltpu.VMEM((quarter, LANES), f32),
                pltpu.VMEM((quarter, LANES), f32),
                dma((4,)), dma((own,)), dma, dma,
                dma((groups + 1, PARTS)), dma((groups, PARTS)), dma((peers,)), dma((peers,)),
                dma((inner - 1,)), dma((inner - 1,)),
                dma((n,)), dma((n,)), dma((n,)), dma((n,)), dma((n,)), dma((n,)),
                dma((n,)), dma((groups * segs,)), dma((4,)), dma((groups,)),
            ],
            compiler_params=pltpu.CompilerParams(
                collective_id=0, has_side_effects=True, vmem_limit_bytes=60 * 1024 * 1024,
            ),
        )(attn_out, w_blocks, w_scales, residual)
        tile = pl.BlockSpec((quarter, my_cols), lambda k: (k, 0))
        return pl.pallas_call(
            finish,
            grid=(4,),
            out_shape=(out, out),
            in_specs=[
                tile,
                pl.BlockSpec((quarter, LANES), lambda k: (k, 0)),
                pl.BlockSpec((1, my_cols), lambda k: (0, 0)),
            ],
            out_specs=(tile, tile),
        )(hidden, scale, gain[None, :])

    return jax.shard_map(
        on_device,
        mesh=mesh,
        in_specs=(
            P("dp", "tensor"),
            P("tensor", "dp"),
            P("tensor", "dp"),
            P("dp", None),
            P("tensor"),
        ),
        out_specs=(P("dp", "tensor"), P("dp", "tensor")),
        check_vma=False,
    )
```

time: 85.8 us -> 87.5 us (1.020)
  Pallas kernels: 80.4 us -> 86.7 us
  other arithmetic: 2.46 us -> 0 us
  local copies, waits for them, and re-layouts: 2.07 us -> 0 us
    pallas_call x0 -> x1, Pallas kernels: none -> 3.58 us  [on_device(): pl.pallas_call(finish, grid=(4,), out_shape=(out, out), in_specs=[tile, p...]
    pallas_call x1, Pallas kernels: 80.4 us -> 83.1 us  [on_device(): pl.pallas_call(functools.partial(kernel, dp, groups), out_shape=(out, jax...]
    convert_element_type x1 -> x0, other arithmetic: 2.46 us -> none  [on_device(): normed = (hidden.astype(f32) * gain[None, :] * scale[:, :1]).astype(bf16)]
    slice x1 -> x0, local copies, waits for them, and re-layouts: 1.09 us -> none  [on_device(): normed = (hidden.astype(f32) * gain[None, :] * scale[:, :1]).astype(bf16)]
    unnamed x5 -> x0, local copies, waits for them, and re-layouts: 0.98 us -> none
where the time goes in v1:
time: 87.5 us; the launch traced here: 87.3 us
  Pallas kernels  86.7 us (99%)
    pallas_call x1, Pallas kernels, on_device(): pl.pallas_call(functools.partial(kernel, dp, groups), out_shape=(out, jax...  83.1 us
    pallas_call x1, Pallas kernels, on_device(): pl.pallas_call(finish, grid=(4,), out_shape=(out, out), in_specs=[tile, p...  3.58 us

profile of v1, /device:TPU:0, one launch (start us, length us, event | category | flops | bytes accessed | tf_op | source)
XLA Modules:
  0.0 87.3 jit_solution(14366370727490298469)
XLA Ops:
  0.6 83.1 %shard_map.68 = (bf16[256,2048]{1,0:T(8,128)(2,1)}, f32[256,128]{1,0:T(8,128)}) custom-call(bf16[256,1024]{1,0:T(8,128)(2,1)} %a_hbm.1, bf16[1024,1024]{1,0:T(8,128)(2,1)} %w_hbm.1, f32[8,1024]{1,0:T(8,128)} %sc_hbm.1, bf16[256,8192]{1,0:T(8,128)(2,1)} %res_hbm.1), custom_call_target="tpu_custom_call" | custom-call | tf_op jit(solution)/shard_map/pallas_call | solution.py:393
  83.8 3.6 %shard_map.69 = (bf16[256,2048]{1,0:T(8,128)(2,1)}, bf16[256,2048]{1,0:T(8,128)(2,1)}) custom-call(bf16[256,2048]{1,0:T(8,128)(2,1)} %get-tuple-element.4.h_ref, f32[256,128]{1,0:T(8,128)} %get-tuple-element.5.scale_ref, f32[1,2048]{1,0:T(1,128)} %bitcast.1), custom_call_target="tpu_custom_call" | custom-call | tf_op jit(solution)/shard_map/pallas_call | solution.py:426

commit v2 on v1

v2 whole, which is shorter than its diff:
```python
import functools

import jax
import jax.numpy as jnp
from jax import lax
from jax.experimental import pallas as pl
from jax.experimental.pallas import tpu as pltpu
from jax.sharding import PartitionSpec as P

MESH = pl.DeviceIdType.MESH
WIDTH = 256
LANES = 128
PARTS = 2
CHUNKS = 8


def plan(dp, groups, cols):
    inner = dp // groups
    width = min(WIDTH, cols)
    pieces = [(0, c, width) for c in range(0, cols, width)]
    own = len(pieces)
    for r in range(1, inner):
        for c in range(0, cols, width):
            if r == inner - 1 and c == cols - width and width > LANES:
                pieces += [(r, k, LANES) for k in range(c, cols, LANES)]
            else:
                pieces.append((r, c, width))
    units = [(j, s) for s in range(len(pieces)) for j in range(groups)]
    return inner, width, pieces, own, units


HOP, SWAP, START, TURN, DOT, CROSS = 11.3, 45.0, 4.5, 1.8, 0.42, 0.7


def steps(dp, groups, cols, middle):
    inner, width, pieces, own, units = plan(dp, groups, cols)
    far = [0, 1, 2, 1] if middle else [0, 1, 2, 3]
    total = sum(w for _, _, w in pieces[own:])
    got, weight = 0, []
    for r, _, w in pieces:
        got += w if r else 0
        weight.append(START + SWAP * got / total if r else 0.0)
    todo = []
    for k in range(1, groups):
        for h in range(PARTS):
            todo.append((START + HOP * (k - 1) + HOP * (h + 1) / PARTS, 0, "pass", k, h))
    token = [START + HOP * far[j] if far[j] else 0.0 for j in range(groups)]
    last = START + HOP * (groups - 1)
    ready = []
    for s in range(len(pieces)):
        if weight[s] >= last - 1:
            ready.append((max(last, weight[s]), -9, s, list(range(groups))[::-1]))
        else:
            ready += [(max(token[j], weight[s]), -far[j], s, [j]) for j in range(groups)]
    free = cross = 0.0
    seen = set()
    sent = START + HOP * 2 + 0.1
    for at, _, s, js in sorted(ready):
        size = pieces[s][2] / WIDTH
        free = max(free, at)
        if s not in seen:
            seen.add(s)
            todo.append((free, 1, "weights", s, 0))
        todo.append((free, 2, "dots" if len(js) > 1 else "dot", s, js))
        free += DOT * size * (1 if len(js) == 1 else 2)
        for j in js:
            u = s * groups + j
            todo.append((free + TURN, 3, "core", u, 0))
            cross = max(cross, free + TURN) + CROSS * size
            out = cross + TURN
            if j > 0 and out < sent:
                out = sent
            todo.append((out, 4, "x", u, 0))
    end = max(e[0] for e in todo)
    for s in range(len(pieces)):
        todo.append((end, 5, "add", s, 0))
    return [(name, u, h) for _, _, name, u, h in sorted(todo, key=lambda e: e[:2])]


def kernel(
    dp, groups,
    a_hbm, w_hbm, sc_hbm, res_hbm,
    hidden, scl,
    a_buf, w_buf, sc_buf, wd, res,
    keep1, snd1, rcv1, snd2, keep2, rcv2, snd3, zin, acc, sums,
    a_load, w_load, sc_load, res_load,
    a_send, a_recv, w_send, w_recv, sc_send, sc_recv,
    s1, r1, s2, r2, s3, r3, s5, r5,
):
    rows, depth = a_hbm.shape
    cols = w_hbm.shape[1]
    my_cols = hidden.shape[1]
    blocks = sc_hbm.shape[0]
    per_block = depth // blocks
    half, quarter = rows // 2, rows // 4
    inner, width, pieces, own, units = plan(dp, groups, cols)
    segs = len(pieces)

    d = lax.axis_index("dp")
    t = lax.axis_index("tensor")
    z, i = d // inner, d % inner
    core, x = t % 2, t // 2
    core_peer = t + 1 - 2 * core
    x_peer = (t + 2) % 4

    def line(o):
        return {"dp": o * inner + i, "tensor": t}

    def row(other):
        return {"dp": d, "tensor": other}

    def pair(other):
        return {"dp": z * inner + other, "tensor": t}

    def step_block(j):
        if j == 0:
            return z
        if j == 1:
            return z + 1 - 2 * (z % 2)
        if j == 2:
            return z + 2 - 4 * (z // 2)
        return 3 - z

    def row_offset(who):
        return pl.multiple_of((who % 2) * half + (who // 2) * quarter, quarter)

    def seg_col(s):
        r, c, w = pieces[s]
        return pl.multiple_of(((i + r) % inner) * cols + c, w)

    def remote(src, dst, send, recv, to):
        return pltpu.make_async_remote_copy(
            src_ref=src, dst_ref=dst, send_sem=send, recv_sem=recv,
            device_id=to, device_id_type=MESH,
        )

    mine = row_offset(t)
    order = [t, x_peer, core_peer, (core_peer + 2) % 4]

    def load_a(q):
        return pltpu.make_async_copy(
            a_hbm.at[pl.ds(row_offset(order[q]), quarter), :],
            a_buf.at[z, pl.ds(q * quarter, quarter), :], a_load.at[q],
        )

    def load_w(s):
        _, c, w = pieces[s]
        return pltpu.make_async_copy(w_hbm.at[:, pl.ds(c, w)], w_buf.at[s, :, pl.ds(0, w)], w_load.at[s])

    sc_copy_in = pltpu.make_async_copy(sc_hbm, sc_buf.at[0], sc_load)
    res_copy = pltpu.make_async_copy(
        res_hbm.at[:, pl.ds(pl.multiple_of(t * my_cols, my_cols), my_cols)], res, res_load
    )
    for q in range(4):
        load_a(q).start()
    sc_copy_in.start()
    for s in range(own):
        load_w(s).start()
    res_copy.start()

    barrier = pltpu.get_barrier_semaphore()
    for r in range(1, inner):
        pl.semaphore_signal(barrier, inc=1, device_id=pair((i + r) % inner), device_id_type=MESH)
    for r in range(1, groups):
        pl.semaphore_signal(barrier, inc=1, device_id=line((z + r) % groups), device_id_type=MESH)
    for r in range(1, 4):
        pl.semaphore_signal(barrier, inc=1, device_id=row((t + r) % 4), device_id_type=MESH)
    pl.semaphore_wait(barrier, inner - 1 + groups - 1 + 3)

    size = rows // PARTS

    def a_copy(block, h, send, to):
        part = a_buf.at[block, pl.ds(h * size, size), :]
        return remote(part, part, a_send.at[send, h], a_recv.at[block, h], line(to))

    def sc_copy(r):
        return remote(sc_buf.at[0], sc_buf.at[r], sc_send.at[r - 1], sc_recv.at[r - 1], pair((i + inner - r) % inner))

    def w_copy(s):
        r, c, w = pieces[s]
        k, at = c // width, c % width
        return remote(
            w_buf.at[k, :, pl.ds(at, w)], w_buf.at[s, :, pl.ds(0, w)], w_send.at[s - own], w_recv.at[s - own],
            pair((i + inner - r) % inner),
        )

    for q in range(4):
        load_a(q).wait()
    for h in range(PARTS):
        @pl.when(z < groups - 1)
        def _():
            a_copy(z, h, z, z + 1).start()

        @pl.when(z > 0)
        def _():
            a_copy(z, h, groups, z - 1).start()

    sc_copy_in.wait()
    for r in range(1, inner):
        sc_copy(r).start()
    landed = set()
    for s in range(own, segs):
        k = pieces[s][1] // width
        if k not in landed:
            landed.add(k)
            load_w(k).wait()
        w_copy(s).start()

    def dequantize(s):
        r, c, w = pieces[s]
        for b in range(blocks):
            lines = pl.ds(b * per_block, per_block)
            raw = w_buf[s, lines, pl.ds(0, w)]
            scale = sc_buf[r, pl.ds(b, 1), pl.ds(c, w)]
            wd[s, lines, pl.ds(0, w)] = (raw.astype(jnp.float32) * scale).astype(jnp.bfloat16)

    def forward(k, h):
        @pl.when(z >= k)
        def _():
            b = z - k
            a_copy(b, h, b, z).wait_recv()

            @pl.when(z < groups - 1)
            def _():
                a_copy(b, h, b, z + 1).start()

        @pl.when(z + k <= groups - 1)
        def _():
            b = z + k
            a_copy(b, h, b, z).wait_recv()

            @pl.when(z > 0)
            def _():
                a_copy(b, h, b, z - 1).start()

    def piece(ref, u):
        return ref.at[u, :, pl.ds(0, pieces[units[u][1]][2])]

    def copy1(u):
        return remote(piece(snd1, u), piece(rcv1, u), s1.at[u], r1.at[u], row(core_peer))

    def copy2(u):
        return remote(piece(snd2, u), piece(rcv2, u), s2.at[u], r2.at[u], row(x_peer))

    def spot(who, s):
        return zin.at[s, pl.ds(row_offset(who), quarter), pl.ds(0, pieces[s][2])]

    def copy3(u):
        j, s = units[u]
        to = {"dp": step_block(j) * inner + i, "tensor": z}
        return remote(piece(snd3, u), spot(t, s), s3.at[u], r3.at[s, t], to)

    def stage1(u):
        j, s = units[u]
        w = pieces[s][2]
        part = jnp.dot(a_buf[step_block(j)], wd[s, :, pl.ds(0, w)], preferred_element_type=jnp.float32)
        snd1[u, :, pl.ds(0, w)] = part[half:].astype(jnp.bfloat16)
        copy1(u).start()
        keep1[u, :, pl.ds(0, w)] = part[:half]

    def stage1_all(s, js):
        w = pieces[s][2]
        tokens = a_buf[...].reshape(groups * rows, depth)
        part = jnp.dot(tokens, wd[s, :, pl.ds(0, w)], preferred_element_type=jnp.float32)
        for b in range(groups):
            u = s * groups + step_block(b)
            snd1[u, :, pl.ds(0, w)] = part[b * rows + half:(b + 1) * rows].astype(jnp.bfloat16)
            keep1[u, :, pl.ds(0, w)] = part[b * rows:b * rows + half]
        for j in js:
            copy1(s * groups + j).start()

    def stage2(u):
        w = pieces[units[u][1]][2]
        copy1(u).wait_recv()
        total = keep1[u, :, pl.ds(0, w)] + rcv1[u, :, pl.ds(0, w)].astype(jnp.float32)
        snd2[u, :, pl.ds(0, w)] = total[quarter:].astype(jnp.bfloat16)
        copy2(u).start()
        keep2[u, :, pl.ds(0, w)] = total[:quarter]

    def stage3(u):
        j, s = units[u]
        w = pieces[s][2]
        copy2(u).wait_recv()
        total = (keep2[u, :, pl.ds(0, w)] + rcv2[u, :, pl.ds(0, w)].astype(jnp.float32)).astype(jnp.bfloat16)
        if j > 0:
            snd3[u, :, pl.ds(0, w)] = total
            copy3(u).start()
        else:
            @pl.when(z == t)
            def _():
                zin[s, pl.ds(mine, quarter), pl.ds(0, w)] = total

            @pl.when(z != t)
            def _():
                snd3[u, :, pl.ds(0, w)] = total
                copy3(u).start()

    def stage4(s):
        w = pieces[s][2]
        for who in range(4):
            @pl.when((z != t) | (t != who))
            def _():
                remote(piece(snd3, s * groups), spot(who, s), s3.at[0], r3.at[s, who], row(who)).wait_recv()
        at = pl.ds(seg_col(s), w)
        h = (zin[s, :, pl.ds(0, w)].astype(jnp.float32) + res[:, at].astype(jnp.float32)).astype(jnp.bfloat16)
        hidden[:, at] = h
        wide = h.astype(jnp.float32)
        square = wide * wide
        total = acc[...]
        for k in range(w // LANES):
            total = total + square[:, k * LANES:(k + 1) * LANES]
        acc[...] = total

    acc[...] = jnp.zeros_like(acc)

    def weights(s):
        r = pieces[s][0]
        if r > 0:
            if pieces[s - 1][0] != r:
                sc_copy(r).wait_recv()
            w_copy(s).wait_recv()
        dequantize(s)

    res_copy.wait()

    def run(middle):
        for name, u, h in steps(dp, groups, cols, middle):
            if name == "pass":
                forward(u, h)
            elif name == "weights":
                weights(u)
            elif name == "dot":
                stage1(u * groups + h[0])
            elif name == "dots":
                stage1_all(u, h)
            elif name == "core":
                stage2(u)
            elif name == "x":
                stage3(u)
            else:
                stage4(u)

    outer = (z == 0) | (z == groups - 1)
    pl.when(outer)(lambda: run(False))
    pl.when(jnp.logical_not(outer))(lambda: run(True))

    exact = lax.Precision.HIGHEST
    sums[t] = lax.dot_general(
        jnp.ones((8, LANES), jnp.float32), acc[...], (((1,), (1,)), ((), ())),
        precision=exact, preferred_element_type=jnp.float32,
    )

    def copy5(r):
        return remote(sums.at[t], sums.at[t], s5.at[r - 1], r5.at[t], row((t + r) % 4))

    for r in range(1, 4):
        copy5(r).start()

    @pl.when(z < groups - 1)
    def _():
        for h in range(PARTS):
            a_copy(z, h, z, z + 1).wait_send()

    @pl.when(z > 0)
    def _():
        for h in range(PARTS):
            a_copy(z, h, groups, z - 1).wait_send()

    for k in range(1, groups):
        @pl.when((z >= k) & (z < groups - 1))
        def _():
            for h in range(PARTS):
                a_copy(z - k, h, z - k, z + 1).wait_send()

        @pl.when((z + k <= groups - 1) & (z > 0))
        def _():
            for h in range(PARTS):
                a_copy(z + k, h, z + k, z - 1).wait_send()

    for r in range(1, inner):
        sc_copy(r).wait_send()
    for s in range(own, segs):
        w_copy(s).wait_send()
    for u, (j, s) in enumerate(units):
        copy1(u).wait_send()
        copy2(u).wait_send()

        @pl.when((z != t) | (j > 0))
        def _():
            copy3(u).wait_send()

    for r in range(1, 4):
        who = (t + r) % 4
        remote(sums.at[t], sums.at[who], s5.at[0], r5.at[who], row(who)).wait_recv()
    for r in range(1, 4):
        copy5(r).wait_send()
    mean_square = (sums[0] + sums[1] + sums[2] + sums[3]) / (my_cols * groups)
    first = (lax.broadcasted_iota(jnp.int32, (8, LANES), 0) == 0).astype(jnp.float32)
    scl[...] = lax.dot_general(
        lax.rsqrt(mean_square + 1e-05), first, (((0,), (0,)), ((), ())),
        precision=exact, preferred_element_type=jnp.float32,
    )


def finish(chunks, h_ref, scale_ref, gain_ref, hidden_hbm, normed_hbm, normed, sems):
    size = h_ref.shape[0] // chunks
    copies = [pltpu.make_async_copy(h_ref, hidden_hbm, sems.at[chunks])]
    copies[0].start()
    for k in range(chunks):
        at = pl.ds(k * size, size)
        wide = h_ref[at, :].astype(jnp.float32)
        normed[at, :] = (wide * gain_ref[...] * scale_ref[at, :1]).astype(jnp.bfloat16)
        copies.append(pltpu.make_async_copy(normed.at[at, :], normed_hbm.at[at, :], sems.at[k]))
        copies[-1].start()
    for copy in copies:
        copy.wait()


def solution(mesh):
    dp, groups = mesh.shape["dp"], mesh.shape["tensor"]

    def on_device(attn_out, w_blocks, w_scales, residual, gain):
        rows, depth = attn_out.shape
        cols = w_blocks.shape[1]
        my_cols = gain.shape[0]
        inner, width, pieces, own, units = plan(dp, groups, cols)
        segs = len(pieces)
        n = len(units)
        peers = segs - own
        half, quarter = rows // 2, rows // 4
        bf16, f32 = jnp.bfloat16, jnp.float32
        hbm = pl.BlockSpec(memory_space=pltpu.MemorySpace.HBM)
        vmem = pl.BlockSpec(memory_space=pltpu.VMEM)
        dma = pltpu.SemaphoreType.DMA
        out = jax.ShapeDtypeStruct((rows, my_cols), bf16)
        hidden, scale = pl.pallas_call(
            functools.partial(kernel, dp, groups),
            out_shape=(out, jax.ShapeDtypeStruct((rows, LANES), f32)),
            in_specs=[hbm] * 4,
            out_specs=(vmem, vmem),
            scratch_shapes=[
                pltpu.VMEM((groups, rows, depth), bf16),
                pltpu.VMEM((segs, depth, width), bf16),
                pltpu.VMEM((inner,) + w_scales.shape, f32),
                pltpu.VMEM((segs, depth, width), bf16),
                pltpu.VMEM((rows, my_cols), bf16),
                pltpu.VMEM((n, half, width), f32),
                pltpu.VMEM((n, half, width), bf16),
                pltpu.VMEM((n, half, width), bf16),
                pltpu.VMEM((n, quarter, width), bf16),
                pltpu.VMEM((n, quarter, width), f32),
                pltpu.VMEM((n, quarter, width), bf16),
                pltpu.VMEM((n, quarter, width), bf16),
                pltpu.VMEM((segs, rows, width), bf16),
                pltpu.VMEM((rows, LANES), f32),
                pltpu.VMEM((groups, 8, rows), f32),
                dma((4,)), dma((own,)), dma, dma,
                dma((groups + 1, PARTS)), dma((groups, PARTS)), dma((peers,)), dma((peers,)),
                dma((inner - 1,)), dma((inner - 1,)),
                dma((n,)), dma((n,)), dma((n,)), dma((n,)), dma((n,)), dma((segs, groups)),
                dma((3,)), dma((groups,)),
            ],
            compiler_params=pltpu.CompilerParams(
                collective_id=0, has_side_effects=True, vmem_limit_bytes=48 * 1024 * 1024,
            ),
        )(*[pltpu.with_memory_space_constraint(v, pltpu.MemorySpace.HBM) for v in (attn_out, w_blocks, w_scales, residual)])
        return pl.pallas_call(
            functools.partial(finish, CHUNKS),
            out_shape=(out, out),
            in_specs=[vmem] * 3,
            out_specs=(hbm, hbm),
            scratch_shapes=[pltpu.VMEM((rows, my_cols), bf16), dma((CHUNKS + 1,))],
            compiler_params=pltpu.CompilerParams(vmem_limit_bytes=16 * 1024 * 1024),
        )(hidden, scale, gain[None, :])

    return jax.shard_map(
        on_device,
        mesh=mesh,
        in_specs=(
            P("dp", "tensor"),
            P("tensor", "dp"),
            P("tensor", "dp"),
            P("dp", None),
            P("tensor"),
        ),
        out_specs=(P("dp", "tensor"), P("dp", "tensor")),
        check_vma=False,
    )
```

time: 87.5 us -> 79 us (0.903)
  Pallas kernels: 86.7 us -> 77.2 us
    pallas_call x1, Pallas kernels: 83.1 us -> 75.8 us  [on_device(): pl.pallas_call(functools.partial(kernel, dp, groups), out_shape=(out, jax...]
    pallas_call x1, Pallas kernels: 3.58 us -> 1.38 us  [on_device(): pl.pallas_call(functools.partial(finish, CHUNKS), out_shape=(out, out), i...]
where the time goes in v2:
time: 79 us; the launch traced here: 78 us
  Pallas kernels  77.2 us (98%)
  between operations  0.84 us (1%)
    pallas_call x1, Pallas kernels, on_device(): pl.pallas_call(functools.partial(kernel, dp, groups), out_shape=(out, jax...  75.8 us

profile of v2, /device:TPU:0, one launch (start us, length us, event | category | flops | bytes accessed | tf_op | source)
XLA Modules:
  0.0 78.0 jit_solution(242388080103639886)
XLA Ops:
  0.6 0.0 copy-start
  0.6 75.8 %shard_map.68 = (bf16[256,2048]{1,0:T(8,128)(2,1)S(1)}, f32[256,128]{1,0:T(8,128)S(1)}) custom-call(bf16[256,1024]{1,0:T(8,128)(2,1)} %a_hbm.1, bf16[1024,1024]{1,0:T(8,128)(2,1)} %w_hbm.1, f32[8,1024]{1,0:T(8,128)} %sc_hbm.1, bf16[256,8192]{1,0:T(8,128)(2,1)} %res_hbm.1), custom_call_target="tpu_custom_call" | custom-call | tf_op jit(solution)/shard_map/pallas_call | solution.py:436
  76.5 0.0 copy-done
  76.5 1.4 %shard_map.69 = (bf16[256,2048]{1,0:T(8,128)(2,1)}, bf16[256,2048]{1,0:T(8,128)(2,1)}) custom-call(bf16[256,2048]{1,0:T(8,128)(2,1)S(1)} %get-tuple-element.4.h_ref, f32[256,128]{1,0:T(8,128)S(1)} %get-tuple-element.5.scale_ref, f32[1,2048]{1,0:T(1,128)S(1)} %bitcast.1), custom_call_target="tpu_custom_call" | custom-call | tf_op jit(solution)/shard_map/pallas_call | solution.py:467
Async XLA Ops:
  0.6 75.8 %copy-start = (f32[2048]{0:T(1024)S(1)}, f32[2048]{0:T(1024)}, u32[]{:S(2)}) copy-start(f32[2048]{0:T(1024)} %param.9) | copy-start | bytes 24580

commit v3 on v2

--- a/solution.py
+++ b/solution.py
@@ -12,6 +12,7 @@
 LANES = 128
 PARTS = 2
 CHUNKS = 8
+WHOLE = 3
 
 
 def plan(dp, groups, cols):
@@ -29,7 +30,11 @@
     return inner, width, pieces, own, units
 
 
-HOP, SWAP, START, TURN, DOT, CROSS = 11.3, 45.0, 4.5, 1.8, 0.42, 0.7
+def direct(groups, own, u, middle):
+    return not middle and u % groups == groups - 1 and u // groups < -(-own * WHOLE // 4)
+
+
+HOP, SWAP, START, TURN, DOT, CROSS, SLACK = 11.3, 45.0, 4.5, 1.8, 0.42, 0.8, 1.0
 
 
 def steps(dp, groups, cols, middle):
@@ -66,8 +71,9 @@
         for j in js:
             u = s * groups + j
             todo.append((free + TURN, 3, "core", u, 0))
-            cross = max(cross, free + TURN) + CROSS * size
-            out = cross + TURN
+            wide = 2 if direct(groups, own, u, middle) else 1
+            cross = max(cross, free + TURN) + CROSS * size * wide
+            out = cross + TURN + SLACK
             if j > 0 and out < sent:
                 out = sent
             todo.append((out, 4, "x", u, 0))
@@ -82,10 +88,10 @@
     a_hbm, w_hbm, sc_hbm, res_hbm,
     hidden, scl,
     a_buf, w_buf, sc_buf, wd, res,
-    keep1, snd1, rcv1, snd2, keep2, rcv2, snd3, zin, acc, sums,
+    keep1, snd1, rcv1, snd2, keep2, rcv2, snd3, sndh, rcvh, zin, acc, sums,
     a_load, w_load, sc_load, res_load,
     a_send, a_recv, w_send, w_recv, sc_send, sc_recv,
-    s1, r1, s2, r2, s3, r3, s5, r5,
+    s1, r1, s2, r2, s3, s3h, r3, s5, r5,
 ):
     rows, depth = a_hbm.shape
     cols = w_hbm.shape[1]
@@ -239,6 +245,18 @@
     def copy1(u):
         return remote(piece(snd1, u), piece(rcv1, u), s1.at[u], r1.at[u], row(core_peer))
 
+    def slot(ref, u):
+        return ref.at[units[u][1], :, pl.ds(0, pieces[units[u][1]][2])]
+
+    def copy2h(u):
+        return remote(slot(sndh, u), slot(rcvh, u), s2.at[u], r2.at[u], row(x_peer))
+
+    def copy3h(u, q):
+        j, s = units[u]
+        to = {"dp": step_block(j) * inner + i, "tensor": z}
+        part = sndh.at[s, pl.ds(q * quarter, quarter), pl.ds(0, pieces[s][2])]
+        return remote(part, spot([t, x_peer][q], s), [s3, s3h][q].at[u], r3.at[s, [t, x_peer][q]], to)
+
     def copy2(u):
         return remote(piece(snd2, u), piece(rcv2, u), s2.at[u], r2.at[u], row(x_peer))
 
@@ -269,17 +287,41 @@
         for j in js:
             copy1(s * groups + j).start()
 
-    def stage2(u):
+    def stage2(u, middle):
         w = pieces[units[u][1]][2]
         copy1(u).wait_recv()
         total = keep1[u, :, pl.ds(0, w)] + rcv1[u, :, pl.ds(0, w)].astype(jnp.float32)
+        if direct(groups, own, u, middle):
+            at = units[u][1]
+
+            @pl.when(x == z // 2)
+            def _():
+                keep1[u, :, pl.ds(0, w)] = total
+
+            @pl.when(x != z // 2)
+            def _():
+                sndh[at, pl.ds(0, quarter), pl.ds(0, w)] = total[quarter:].astype(jnp.bfloat16)
+                sndh[at, pl.ds(quarter, quarter), pl.ds(0, w)] = total[:quarter].astype(jnp.bfloat16)
+                copy2h(u).start()
+
+            return
         snd2[u, :, pl.ds(0, w)] = total[quarter:].astype(jnp.bfloat16)
         copy2(u).start()
         keep2[u, :, pl.ds(0, w)] = total[:quarter]
 
-    def stage3(u):
+    def stage3(u, middle):
         j, s = units[u]
         w = pieces[s][2]
+        if direct(groups, own, u, middle):
+            @pl.when(x == z // 2)
+            def _():
+                copy2h(u).wait_recv()
+                both = keep1[u, :, pl.ds(0, w)] + rcvh[s, :, pl.ds(0, w)].astype(jnp.float32)
+                sndh[s, :, pl.ds(0, w)] = both.astype(jnp.bfloat16)
+                for q in range(2):
+                    copy3h(u, q).start()
+
+            return
         copy2(u).wait_recv()
         total = (keep2[u, :, pl.ds(0, w)] + rcv2[u, :, pl.ds(0, w)].astype(jnp.float32)).astype(jnp.bfloat16)
         if j > 0:
@@ -334,9 +376,9 @@
             elif name == "dots":
                 stage1_all(u, h)
             elif name == "core":
-                stage2(u)
+                stage2(u, middle)
             elif name == "x":
-                stage3(u)
+                stage3(u, middle)
             else:
                 stage4(u)
 
@@ -383,11 +425,27 @@
         w_copy(s).wait_send()
     for u, (j, s) in enumerate(units):
         copy1(u).wait_send()
-        copy2(u).wait_send()
-
-        @pl.when((z != t) | (j > 0))
-        def _():
-            copy3(u).wait_send()
+
+        def plain(u=u, j=j):
+            copy2(u).wait_send()
+
+            @pl.when((z != t) | (j > 0))
+            def _():
+                copy3(u).wait_send()
+
+        if direct(groups, own, u, False):
+            @pl.when(outer & (x == z // 2))
+            def _():
+                for q in range(2):
+                    copy3h(u, q).wait_send()
+
+            @pl.when(outer & (x != z // 2))
+            def _():
+                copy2h(u).wait_send()
+
+            pl.when(jnp.logical_not(outer))(plain)
+        else:
+            plain()
 
     for r in range(1, 4):
         who = (t + r) % 4
@@ -451,13 +509,15 @@
                 pltpu.VMEM((n, quarter, width), f32),
                 pltpu.VMEM((n, quarter, width), bf16),
                 pltpu.VMEM((n, quarter, width), bf16),
+                pltpu.VMEM((-(-own * WHOLE // 4), half, width), bf16),
+                pltpu.VMEM((-(-own * WHOLE // 4), half, width), bf16),
                 pltpu.VMEM((segs, rows, width), bf16),
                 pltpu.VMEM((rows, LANES), f32),
                 pltpu.VMEM((groups, 8, rows), f32),
                 dma((4,)), dma((own,)), dma, dma,
                 dma((groups + 1, PARTS)), dma((groups, PARTS)), dma((peers,)), dma((peers,)),
                 dma((inner - 1,)), dma((inner - 1,)),
-                dma((n,)), dma((n,)), dma((n,)), dma((n,)), dma((n,)), dma((segs, groups)),
+                dma((n,)), dma((n,)), dma((n,)), dma((n,)), dma((n,)), dma((n,)), dma((segs, groups)),
                 dma((3,)), dma((groups,)),
             ],
             compiler_params=pltpu.CompilerParams(

time: 79 us -> 73.2 us (0.927); the launches traced: 78 us -> 73.1 us
  Pallas kernels: 77.2 us -> 72.3 us
    pallas_call x1, Pallas kernels: 75.8 us -> 70.9 us  [on_device(): pl.pallas_call(functools.partial(kernel, dp, groups), out_shape=(out, jax...]
where the time goes in v3:
time: 73.2 us; the launch traced here: 73.1 us
  Pallas kernels  72.3 us (99%)
  between operations  0.84 us (1%)
    pallas_call x1, Pallas kernels, on_device(): pl.pallas_call(functools.partial(kernel, dp, groups), out_shape=(out, jax...  70.9 us

profile of v3, /device:TPU:0, one launch (start us, length us, event | category | flops | bytes accessed | tf_op | source)
XLA Modules:
  0.0 73.1 jit_solution(6917473693684982905)
XLA Ops:
  0.6 0.0 copy-start
  0.6 70.9 %shard_map.68 = (bf16[256,2048]{1,0:T(8,128)(2,1)S(1)}, f32[256,128]{1,0:T(8,128)S(1)}) custom-call(bf16[256,1024]{1,0:T(8,128)(2,1)} %a_hbm.1, bf16[1024,1024]{1,0:T(8,128)(2,1)} %w_hbm.1, f32[8,1024]{1,0:T(8,128)} %sc_hbm.1, bf16[256,8192]{1,0:T(8,128)(2,1)} %res_hbm.1), custom_call_target="tpu_custom_call" | custom-call | tf_op jit(solution)/shard_map/pallas_call | solution.py:494
  71.5 0.0 copy-done
  71.5 1.4 %shard_map.69 = (bf16[256,2048]{1,0:T(8,128)(2,1)}, bf16[256,2048]{1,0:T(8,128)(2,1)}) custom-call(bf16[256,2048]{1,0:T(8,128)(2,1)S(1)} %get-tuple-element.4.h_ref, f32[256,128]{1,0:T(8,128)S(1)} %get-tuple-element.5.scale_ref, f32[1,2048]{1,0:T(1,128)S(1)} %bitcast.1), custom_call_target="tpu_custom_call" | custom-call | tf_op jit(solution)/shard_map/pallas_call | solution.py:527
Async XLA Ops:
  0.6 70.9 %copy-start = (f32[2048]{0:T(1024)S(1)}, f32[2048]{0:T(1024)}, u32[]{:S(2)}) copy-start(f32[2048]{0:T(1024)} %param.9) | copy-start | bytes 24580
